TPU v7x, 256 devices: a whole 4x4x8 slice. The times are simulated.
256 devices in a mesh: band: 32 (over z, y_hi, core), chan: 8 (over x, y_lo).
Axes of the slice: x: 4, y: 4 (y_hi: 2, y_lo: 2; y = y_hi * 2 + y_lo), z: 8, core: 2. Of those that a mesh axis runs over, the one named last changes fastest.
Arguments:
- fine_features: bfloat16 [2, 192, 256, 512], P(None, 'chan', 'band'), may hold values from -100 to 100
- coarse_level: bfloat16 [2, 256, 128, 256], P(None, 'chan', 'band'), may hold values from -100 to 100
- lat_weight: bfloat16 [256, 192], P('chan'), may hold values from -0.4375 to 0.4375
- lat_gain: bfloat16 [256], P('chan'), may hold values from 0.099609375 to 1.8984375
- lat_shift: bfloat16 [256], P('chan'), may hold values from -3 to 3
- out_weight: bfloat16 [3, 3, 256, 256], P(None, None, 'chan'), may hold values from -0.125 to 0.125
- out_gain: bfloat16 [256], P('chan'), may hold values from 0.099609375 to 1.8984375
- out_shift: bfloat16 [256], P('chan'), may hold values from -3 to 3
- mask_weight: bfloat16 [256, 256], P('chan'), may hold values from -0.375 to 0.375
- mask_bias: bfloat16 [256], P('chan'), may hold values from -1.796875 to 1.796875
- queries: bfloat16 [200, 256], replicated, may hold values from -128 to 128
Outputs:
- log_probs: float32 [2, 200, 256, 512], P(None, None, ('band', 'chan'))
All inputs are finite; a program needn't handle non-finite values.
Results may differ from a plain program's by a relative error of at most 0.0058.
Values may be sent and summed in bfloat16 or wider, within the bound.
A program may use at most 64 MiB of HBM per device.

v0:
```python
import functools
import jax
import jax.numpy as jnp
from jax import lax
from jax.sharding import Mesh
from jax.sharding import PartitionSpec as P

D = 256
GROUPS = 32
BAND = ("band_0", "band_1", "band_2")
CHAN = ("chan_0", "chan_1")
BAND_CHAN = ("band_0", "band_1", "band_2", "chan_0", "chan_1")
epsilon = 1e-05


def whole_of(shard, axes, dim):
    for axis in reversed(axes):
        shard = lax.all_gather(shard, axis, axis=dim, tiled=True)
    return shard


def from_everyone(shard, axis):
    devices = lax.axis_size(axis)
    return lax.all_to_all(
        jnp.broadcast_to(shard[None], (devices, *shard.shape)), axis, 0, 0, tiled=True
    )


def of_everyone(shard, axis):
    everything = from_everyone(shard, axis)
    return jnp.sum(everything, axis=0)


def together(arrays, axis):
    vector, at, done = (jnp.concatenate([a.reshape(-1) for a in arrays]), 0, [])
    total = of_everyone(vector, axis)
    for a in arrays:
        done.append(total[at : at + a.size].reshape(a.shape))
        at += a.size
    return tuple(done)


def extended_2(cells, sides, width):
    for axis, dim in sides:
        count = lax.axis_size(axis)
        ends = count - 1
        head = lax.slice_in_dim(cells, 0, width, axis=dim)
        tail = lax.slice_in_dim(cells, cells.shape[dim] - width, cells.shape[dim], axis=dim)
        cells = jnp.concatenate(
            [
                lax.ppermute(tail, axis, [(i, (i + 1) % count) for i in range(ends)]),
                cells,
                lax.ppermute(head, axis, [((i + 1) % count, i) for i in range(ends)]),
            ],
            axis=dim,
        )
    return cells


def rows_first(arrays, axis, dims):
    turned = [jnp.moveaxis(a, dim, 0) for a, dim in zip(arrays, dims)]
    both = jnp.concatenate([t.reshape(len(t), -1) for t in turned], axis=1)
    result, at, done = (lax.all_gather(both, axis, axis=0, tiled=True), 0, [])
    for t, dim in zip(turned, dims):
        slab = result[:, at : at + t[0].size].reshape(-1, *t.shape[1:])
        done.append(jnp.moveaxis(slab, 0, dim))
        at += t[0].size
    return tuple(done)


def extended_3(shard, sides, width):
    edges = {}
    for axis, dim in sides:
        devices, length = (lax.axis_size(axis), shard.shape[dim])
        up = [(i, (i + 1) % devices) for i in range(devices - 1)]
        last = lax.slice_in_dim(shard, length - width, length, axis=dim)
        first = lax.slice_in_dim(shard, 0, width, axis=dim)
        edges[dim] = (
            lax.ppermute(last, axis, up),
            lax.ppermute(first, axis, [(b, a) for a, b in up]),
        )
    done = []
    for _, dim in sides:
        low, high = edges[dim]
        around = [(width, width) if d in done else (0, 0) for d in range(shard.ndim)]
        shard = jnp.concatenate([jnp.pad(low, around), shard, jnp.pad(high, around)], axis=dim)
        done.append(dim)
    return shard


def over_axes_2(shard, axes):
    return functools.reduce(lax.psum, axes, shard)


def interp(padded, axis):
    length = padded.shape[axis] - 2
    before = lax.slice_in_dim(padded, 0, length, axis=axis)
    middle = lax.slice_in_dim(padded, 1, length + 1, axis=axis)
    after = lax.slice_in_dim(padded, 2, length + 2, axis=axis)
    even_part = 0.25 * before + 0.75 * middle
    odd_part = 0.75 * middle + 0.25 * after
    paired = jnp.stack([even_part, odd_part], axis + 1)
    new_shape = list(middle.shape)
    new_shape[axis] = 2 * length
    return paired.reshape(new_shape)


def conv_taps(taps_weight, padded, row_count, col_count):
    summed = None
    for row_tap in range(3):
        for col_tap in range(3):
            window = padded[:, :, row_tap : row_tap + row_count, col_tap : col_tap + col_count]
            term = jnp.einsum(
                "oc,ncrw->norw",
                taps_weight[row_tap, col_tap],
                window,
                preferred_element_type=jnp.float32,
            )
            summed = term if summed is None else summed + term
    return summed


def apply_norm(blocks, mean_value, variance, full_shape, gain, shift):
    scaled = (
        (blocks - mean_value[:, :, None]) * lax.rsqrt(variance[:, :, None] + epsilon)
    ).reshape(full_shape)
    return (
        scaled * gain.astype(jnp.float32)[None, :, None, None]
        + shift.astype(jnp.float32)[None, :, None, None]
    )


def per_device(
    fine_features,
    coarse_level,
    lat_weight,
    lat_gain,
    lat_shift,
    out_weight,
    out_gain,
    out_shift,
    mask_weight,
    mask_bias,
    queries,
):
    images, in_share, band_rows, columns = fine_features.shape
    out_share = lat_weight.shape[0]
    group_size = D // GROUPS
    band_count = lax.axis_size(BAND)
    pixel_count = float(group_size * band_rows * band_count * columns)
    lateral = jnp.einsum(
        "oc,ncrw->norw",
        lat_weight,
        whole_of(fine_features, CHAN, 1),
        preferred_element_type=jnp.float32,
    )
    lat_blocks = lateral.reshape(images, out_share // group_size, -1)
    first_sum, square_sum = together(
        (jnp.sum(lat_blocks, 2), jnp.sum(lat_blocks * lat_blocks, 2)), BAND
    )
    lat_mean = first_sum / pixel_count
    lat_var = square_sum / pixel_count - lat_mean * lat_mean
    lat_normed = apply_norm(lat_blocks, lat_mean, lat_var, lateral.shape, lat_gain, lat_shift)
    band_index = lax.axis_index(BAND)
    extended = extended_2(coarse_level, ((BAND, 2),), 1)
    top_row = jnp.where(band_index == 0, extended[:, :, 1:2], extended[:, :, 0:1])
    bottom_row = jnp.where(band_index == band_count - 1, extended[:, :, -2:-1], extended[:, :, -1:])
    extended = jnp.concatenate([top_row, extended[:, :, 1:-1], bottom_row], 2).astype(jnp.float32)
    extended = jnp.pad(extended, ((0, 0), (0, 0), (0, 0), (1, 1)), mode="edge")
    upsampled = interp(interp(extended, 2), 3)
    joined = (lat_normed + upsampled).astype(jnp.bfloat16)
    row_joined = lax.all_to_all(joined, CHAN, split_axis=2, concat_axis=1, tiled=True)
    conv_weight, full_gain, full_shift, full_mask, full_bias = rows_first(
        (out_weight, out_gain, out_shift, mask_weight, mask_bias), CHAN, (2, 0, 0, 0, 0)
    )
    row_count = row_joined.shape[2]
    padded = extended_3(row_joined, ((BAND_CHAN, 2),), 1)
    padded = jnp.pad(padded, ((0, 0), (0, 0), (0, 0), (1, 1)))
    conv_out = conv_taps(conv_weight, padded, row_count, columns)
    local_groups = conv_out.shape[1] // group_size
    conv_blocks = conv_out.reshape(images, local_groups, -1)
    first_sum, square_sum = (
        over_axes_2(jnp.sum(conv_blocks, 2), BAND_CHAN),
        over_axes_2(jnp.sum(conv_blocks * conv_blocks, 2), BAND_CHAN),
    )
    out_mean = first_sum / pixel_count
    out_var = square_sum / pixel_count - out_mean * out_mean
    activated = jnp.maximum(
        apply_norm(conv_blocks, out_mean, out_var, conv_out.shape, full_gain, full_shift), 0.0
    ).astype(jnp.bfloat16)
    mixed = jnp.einsum("oc,ncrw->norw", full_mask, activated, preferred_element_type=jnp.float32)
    features = (mixed + full_bias.astype(jnp.float32)[None, :, None, None]).astype(jnp.bfloat16)
    logits = jnp.einsum("qc,ncrw->nqrw", queries, features, preferred_element_type=jnp.float32)
    peak = jnp.max(logits, axis=1, keepdims=True)
    shifted = logits - peak
    return shifted - jnp.log(jnp.sum(jnp.exp(shifted), axis=1, keepdims=True))


def solution(mesh):
    finer = Mesh(
        mesh.devices.reshape(8, 2, 2, 4, 2), ("band_0", "band_1", "band_2", "chan_0", "chan_1")
    )
    return jax.shard_map(
        per_device,
        mesh=finer,
        in_specs=(
            P(None, CHAN, BAND, None),
            P(None, CHAN, BAND, None),
            P(CHAN, None),
            P(CHAN),
            P(CHAN),
            P(None, None, CHAN, None),
            P(CHAN),
            P(CHAN),
            P(CHAN, None),
            P(CHAN),
            P(),
        ),
        out_specs=P(None, None, BAND_CHAN, None),
        check_vma=False,
    )
```

profile of v0, /device:TPU:16, one launch (start us, length us, event | category | flops | bytes accessed | tf_op | source)
XLA Modules:
  0.0 195.7 jit_solution(14821775544528148993)
XLA Ops:
  6.6 1.3 copy.111
  7.9 11.8 %all_gather.9 = bf16[2,48,8,512]{3,1,2,0:T(8,128)(2,1)} all-gather(bf16[2,24,8,512]{3,1,2,0:T(8,128)(2,1)S(1)} %copy.111), channel_id=1, replica_groups=mesh['band_0'=8,'band_1'=2,'band_2'=2,'chan_0'=4,'chan_1'=2] {'chan_1'}, dimensions={1}, use_global_device_ids=true | all-gather | bytes 1179648 | tf_op jit(solution)/shard_map/all_gather | solution.py:18
  19.8 1.9 collective-permute-start
  21.7 5.1 %collective-permute-start.1 = (bf16[2,32,1,256]{3,1,2,0:T(8,128)(2,1)S(1)}, bf16[2,32,1,256]{3,1,2,0:T(8,128)(2,1)S(1)}, u32[]{:S(2)}, u32[]{:S(2)}) collective-permute-start(bf16[2,32,1,256]{3,1,2,0:T(8,128)(2,1)S(1)} %get-tuple-element.31), channel_id=1, source_target_pairs={{8,0},{16,8},{24,16},{32,24},{40,32},{48,40},{56,48},{64,56},{72,6... | collective-permute-start | bytes 98312 | tf_op jit(solution)/shard_map/ppermute | solution.py:53
  26.9 0.1 copy.127
  27.0 0.1 copy.128
  27.1 0.1 copy.129
  27.2 0.1 copy.126
  27.3 0.2 reshape.197
  27.5 0.8 concatenate.20
  28.5 0.1 fusion.51
  28.6 0.3 pad_maximum_fusion.2
  28.9 0.1 fusion.43
  29.1 0.3 fusion.24
  29.4 35.2 %all-gather.3.cloned.1.call-done = bf16[2,192,8,512]{3,1,2,0:T(8,128)(2,1)} async-done(((bf16[2,48,8,512]{3,1,2,0:T(8,128)(2,1)}), bf16[2,192,8,512]{3,1,2,0:T(8,128)(2,1)}) %all-gather.3.cloned.1.call-update) | async-done | bytes 3145744 | tf_op jit(solution)/shard_map/all_gather | solution.py:18
  64.6 2.7 %fusion.50 = (f32[2,32]{1,0:T(2,128)S(1)}, f32[2,32]{1,0:T(2,128)S(1)}, f32[2,32,8,512]{3,1,2,0:T(8,128)S(1)}) fusion(bf16[2,192,8,512]{3,1,2,0:T(8,128)(2,1)} %all-gather.3.cloned.1.call-done, bf16[32,192]{1,0:T(8,128)(2,1)S(1)} %copy-done.5), kind=kOutput, calls=%fused_computation.91 | convolution fusion | flops 101449600 | bytes 4207104 | tf_op jit(solution)/shard_map/oc,ncrw->norw/dot_general | solution.py:151
  67.4 0.1 reduce_sum.67
  67.5 0.1 reshape.192
  67.7 0.1 reduce_sum.73
  67.7 0.1 reshape.193
  67.9 0.6 broadcast_in_dim.2
  68.5 10.1 %all-to-all-start = ((f32[32,1,16]{2,1,0:T(1,128)}), f32[32,1,16]{2,1,0:T(1,128)S(1)}, u32[]{:S(2)}, u32[]{:S(2)}) async-start(f32[32,1,16]{2,1,0:T(1,128)} %broadcast_in_dim.2), calls=%async_computation | async-start | bytes 32768 | tf_op jit(solution)/shard_map/all_to_all | solution.py:24
  78.7 0.1 pad_maximum_fusion
  78.8 3.7 %copy.119 = f32[2,32,8,256,2]{1,2,4,3,0:T(8,128)} copy(f32[2,32,8,256,2]{3,1,2,0,4:T(8,128)S(1)} %pad_maximum_fusion) | data formatting | bytes 2097152 | tf_op jit(solution)/shard_map/stack | solution.py:102
  82.4 2.8 %copy.120 = f32[2,32,8,512]{3,1,2,0:T(8,128)S(1)} copy(f32[2,32,8,512]{1,2,3,0:T(8,128)} %bitcast.154) | data formatting | bytes 2097152 | tf_op jit(solution)/shard_map/reshape | solution.py:105
  85.3 0.5 all-to-all-done
  86.1 0.1 sub.54
  86.3 0.1 mul.92
  86.4 0.4 add_convert_fusion
  86.8 14.9 %all_to_all.24 = bf16[2,32,8,512]{3,1,0,2:T(8,128)(2,1)S(1)} all-to-all(bf16[2,32,8,512]{3,1,0,2:T(8,128)(2,1)S(1)} %copy.121), channel_id=1, replica_groups=mesh['band_0'=8,'band_1'=2,'band_2'=2,'chan_0'=4,'chan_1'=2] {'chan_0','..., dimensions={2} | all-to-all | bytes 1048576 | tf_op jit(solution)/shard_map/all_to_all | solution.py:172
  101.7 1.0 copy.123
  102.7 5.3 %collective-permute-start.3 = (bf16[2,256,1,512]{1,3,0,2:T(8,128)(2,1)}, bf16[2,256,1,512]{1,3,0,2:T(8,128)(2,1)}, u32[]{:S(2)}, u32[]{:S(2)}) collective-permute-start(bf16[2,256,1,512]{1,3,0,2:T(8,128)(2,1)} %copy.123), channel_id=1, source_target_pairs={{1,0},{2,1},{3,2},{4,3},{5,4},{6,5},{7,6},{8,7},{9,8},{10,9},{11,1... | collective-permute-start | bytes 1572872 | tf_op jit(solution)/shard_map/ppermute | solution.py:80
  108.0 1.9 collective-permute-start.2
  110.0 18.9 %all-gather.5.cloned.1.call-done = bf16[256,2563]{1,0:T(8,128)(2,1)} async-done(((bf16[32,2563]{1,0:T(8,128)(2,1)}), bf16[256,2563]{1,0:T(8,128)(2,1)}) %all-gather.5.cloned.1.call-update) | async-done | bytes 1312272 | tf_op jit(solution)/shard_map/all_gather | solution.py:63
  128.9 1.3 slice-done
  130.2 0.6 copy.130
  130.8 1.6 copy.131
  132.4 0.2 convert_reduce_fusion.2
  132.6 1.3 fusion.44
  133.9 0.8 collective-permute-done.2
  134.7 1.7 fusion.5
  136.4 0.3 fusion.17
  136.7 0.3 fusion.18
  137.1 0.3 fusion.19
  137.4 0.3 fusion.20
  137.8 0.3 fusion.16
  138.1 1.4 fusion.27
  139.5 1.4 fusion.25
  140.8 1.6 fusion.49
  142.5 0.1 reduce_sum.90
  142.6 0.1 reduce_sum.91
  142.7 0.1 reduce_sum.93
  142.8 0.1 reduce_sum.94
  142.8 17.4 %all-reduce.1 = (f32[2,32]{1,0:T(2,128)S(1)}, f32[2,32]{1,0:T(2,128)S(1)}) all-reduce(f32[2,32]{1,0:T(2,128)S(1)} %reduce_sum.94, f32[2,32]{1,0:T(2,128)S(1)} %reduce_sum.91), channel_id=1, replica_groups=mesh['band_0'=8,'band_1'=2,'band_2'=2,'chan_0'=4,'chan_1'=2] {'band_0'}, use_global_device_ids=true, to_apply=%region_14.15 | all-reduce | flops 128 | bytes 1024 | tf_op jit(solution)/shard_map/psum | solution.py:92
  160.3 6.4 %all-reduce.5 = (f32[2,32]{1,0:T(2,128)S(1)}, f32[2,32]{1,0:T(2,128)S(1)}) all-reduce(f32[2,32]{1,0:T(2,128)S(1)} %get-tuple-element.12, f32[2,32]{1,0:T(2,128)S(1)} %get-tuple-element.13), channel_id=1, replica_groups=mesh['band_0'=8,'band_1'=2,'band_2'=2,'chan_0'=4,'chan_1'=2] {'band_1'}, use_global_device_ids=true, to_apply=%region_15.16 | all-reduce | flops 128 | bytes 1024 | tf_op jit(solution)/shard_map/psum | solution.py:92
  166.7 2.4 %all-reduce.4 = (f32[2,32]{1,0:T(2,128)S(1)}, f32[2,32]{1,0:T(2,128)S(1)}) all-reduce(f32[2,32]{1,0:T(2,128)S(1)} %get-tuple-element.20, f32[2,32]{1,0:T(2,128)S(1)} %get-tuple-element.21), channel_id=1, replica_groups=mesh['band_0'=8,'band_1'=2,'band_2'=2,'chan_0'=4,'chan_1'=2] {'band_2'}, use_global_device_ids=true, to_apply=%region_16.17 | all-reduce | flops 128 | bytes 1024 | tf_op jit(solution)/shard_map/psum | solution.py:92
  169.1 10.5 %all-reduce.2 = (f32[2,32]{1,0:T(2,128)S(1)}, f32[2,32]{1,0:T(2,128)S(1)}) all-reduce(f32[2,32]{1,0:T(2,128)S(1)} %get-tuple-element.18, f32[2,32]{1,0:T(2,128)S(1)} %get-tuple-element.19), channel_id=1, replica_groups=mesh['band_0'=8,'band_1'=2,'band_2'=2,'chan_0'=4,'chan_1'=2] {'chan_0'}, use_global_device_ids=true, to_apply=%region_17.18 | all-reduce | flops 128 | bytes 1024 | tf_op jit(solution)/shard_map/psum | solution.py:92
  179.6 4.9 %all-reduce.3 = (f32[2,32]{1,0:T(2,128)S(1)}, f32[2,32]{1,0:T(2,128)S(1)}) all-reduce(f32[2,32]{1,0:T(2,128)S(1)} %get-tuple-element.14, f32[2,32]{1,0:T(2,128)S(1)} %get-tuple-element.15), channel_id=1, replica_groups=mesh['band_0'=8,'band_1'=2,'band_2'=2,'chan_0'=4,'chan_1'=2] {'chan_1'}, use_global_device_ids=true, to_apply=%region_18.19 | all-reduce | flops 128 | bytes 1024 | tf_op jit(solution)/shard_map/psum | solution.py:92
  184.6 0.1 sub.59
  184.8 0.1 mul.108
  184.9 1.9 fusion.53
  186.8 0.1 exponential_reduce_fusion
  187.0 0.1 subtract_subtract_fusion
  187.1 1.7 copy.134
  (55 shorter events, 1.3 us)
Async XLA Ops:
  6.5 178.3 %copy-start = (bf16[200,256]{1,0:T(8,128)(2,1)S(1)}, bf16[200,256]{1,0:T(8,128)(2,1)}, u32[]{:S(2)}) copy-start(bf16[200,256]{1,0:T(8,128)(2,1)} %param.21) | copy-start | bytes 307204
  6.5 13.2 %copy-start.4 = (bf16[2,32,4,256]{3,2,1,0:T(4,128)(2,1)S(1)}, bf16[2,32,4,256]{3,2,1,0:T(4,128)(2,1)}, u32[]{:S(2)}) copy-start(bf16[2,32,4,256]{3,2,1,0:T(4,128)(2,1)} %param.12) | copy-start | bytes 393220
  6.5 20.3 %copy-start.7 = (bf16[32]{0:T(256)(128)(2,1)S(1)}, bf16[32]{0:T(256)(128)(2,1)}, u32[]{:S(2)}) copy-start(bf16[32]{0:T(256)(128)(2,1)} %param.17) | copy-start | bytes 196
  6.5 20.4 %copy-start.8 = (bf16[32]{0:T(256)(128)(2,1)S(1)}, bf16[32]{0:T(256)(128)(2,1)}, u32[]{:S(2)}) copy-start(bf16[32]{0:T(256)(128)(2,1)} %param.18) | copy-start | bytes 196
  6.5 20.5 %copy-start.9 = (bf16[32]{0:T(256)(128)(2,1)S(1)}, bf16[32]{0:T(256)(128)(2,1)}, u32[]{:S(2)}) copy-start(bf16[32]{0:T(256)(128)(2,1)} %param.20) | copy-start | bytes 196
  6.5 20.6 %copy-start.3 = (bf16[3,3,32,256]{3,2,1,0:T(8,128)(2,1)S(1)}, bf16[3,3,32,256]{3,2,1,0:T(8,128)(2,1)}, u32[]{:S(2)}) copy-start(bf16[3,3,32,256]{3,2,1,0:T(8,128)(2,1)} %param.16) | copy-start | bytes 442372
  6.6 58.1 %all-gather.3.cloned.1.call-start = ((), (), s32[]{:S(2)}) async-start(), calls=%async_computation.2 | async-start | bytes 3932160 | tf_op jit(solution)/shard_map/all_gather | solution.py:18
  7.9 19.6 %copy-start.6 = (bf16[32,256]{1,0:T(8,128)(2,1)S(1)}, bf16[32,256]{1,0:T(8,128)(2,1)}, u32[]{:S(2)}) copy-start(bf16[32,256]{1,0:T(8,128)(2,1)} %param.19) | copy-start | bytes 49156
  7.9 20.4 %copy-start.10 = (bf16[32]{0:T(256)(128)(2,1)S(1)}, bf16[32]{0:T(256)(128)(2,1)}, u32[]{:S(2)}) copy-start(bf16[32]{0:T(256)(128)(2,1)} %param.14) | copy-start | bytes 196
  7.9 20.4 %copy-start.11 = (bf16[32]{0:T(256)(128)(2,1)S(1)}, bf16[32]{0:T(256)(128)(2,1)}, u32[]{:S(2)}) copy-start(bf16[32]{0:T(256)(128)(2,1)} %param.15) | copy-start | bytes 196
  19.7 109.2 %all-gather.5.cloned.1.call-start = ((), (), s32[]{:S(2)}) async-start(), calls=%async_computation.3 | async-start | bytes 1548288 | tf_op jit(solution)/shard_map/all_gather | solution.py:63
  19.8 8.6 %collective-permute-start = (bf16[2,32,1,256]{3,1,2,0:T(8,128)(2,1)S(1)}, bf16[2,32,1,256]{3,1,2,0:T(8,128)(2,1)S(1)}, u32[]{:S(2)}, u32[]{:S(2)}) collective-permute-start(bf16[2,32,1,256]{3,1,2,0:T(8,128)(2,1)S(1)} %get-tuple-element.30), channel_id=1, source_target_pairs={{0,8},{8,16},{16,24},{24,32},{32,40},{40,48},{48,56},{56,64},{64,7... | collective-permute-start | bytes 98312 | tf_op jit(solution)/shard_map/ppermute | solution.py:51
  21.7 6.7 %collective-permute-start.1 = (bf16[2,32,1,256]{3,1,2,0:T(8,128)(2,1)S(1)}, bf16[2,32,1,256]{3,1,2,0:T(8,128)(2,1)S(1)}, u32[]{:S(2)}, u32[]{:S(2)}) collective-permute-start(bf16[2,32,1,256]{3,1,2,0:T(8,128)(2,1)S(1)} %get-tuple-element.31), channel_id=1, source_target_pairs={{8,0},{16,8},{24,16},{32,24},{40,32},{48,40},{56,48},{64,56},{72,6... | collective-permute-start | bytes 98312 | tf_op jit(solution)/shard_map/ppermute | solution.py:53
  29.1 35.6 %copy-start.5 = (bf16[32,192]{1,0:T(8,128)(2,1)S(1)}, bf16[32,192]{1,0:T(8,128)(2,1)}, u32[]{:S(2)}) copy-start(bf16[32,192]{1,0:T(8,128)(2,1)} %param.13) | copy-start | bytes 36868
  68.5 17.2 %all-to-all-start = ((f32[32,1,16]{2,1,0:T(1,128)}), f32[32,1,16]{2,1,0:T(1,128)S(1)}, u32[]{:S(2)}, u32[]{:S(2)}) async-start(f32[32,1,16]{2,1,0:T(1,128)} %broadcast_in_dim.2), calls=%async_computation | async-start | bytes 32768 | tf_op jit(solution)/shard_map/all_to_all | solution.py:24
  102.7 31.1 %collective-permute-start.3 = (bf16[2,256,1,512]{1,3,0,2:T(8,128)(2,1)}, bf16[2,256,1,512]{1,3,0,2:T(8,128)(2,1)}, u32[]{:S(2)}, u32[]{:S(2)}) collective-permute-start(bf16[2,256,1,512]{1,3,0,2:T(8,128)(2,1)} %copy.123), channel_id=1, source_target_pairs={{1,0},{2,1},{3,2},{4,3},{5,4},{6,5},{7,6},{8,7},{9,8},{10,9},{11,1... | collective-permute-start | bytes 1572872 | tf_op jit(solution)/shard_map/ppermute | solution.py:80
  108.0 26.6 %collective-permute-start.2 = (bf16[2,256,1,512]{1,3,0,2:T(8,128)(2,1)}, bf16[2,256,1,512]{1,3,0,2:T(8,128)(2,1)}, u32[]{:S(2)}, u32[]{:S(2)}) collective-permute-start(bf16[2,256,1,512]{1,3,0,2:T(8,128)(2,1)} %copy.123), channel_id=1, source_target_pairs={{0,1},{1,2},{2,3},{3,4},{4,5},{5,6},{6,7},{7,8},{8,9},{9,10},{10,1... | collective-permute-start | bytes 1572872 | tf_op jit(solution)/shard_map/ppermute | solution.py:79
  128.9 1.3 slice-start
  130.8 1.6 copy-start.1
  133.8 2.6 %copy-start.2 = (bf16[256,3,3,256]{3,0,2,1:T(8,128)(2,1)S(1)}, bf16[256,3,3,256]{3,0,2,1:T(8,128)(2,1)}, u32[]{:S(2)}) copy-start(bf16[256,3,3,256]{3,0,2,1:T(8,128)(2,1)} %copy.131) | copy-start | bytes 3538948
Sparse Core Ops, SparseCore 0:
  19.8 44.7 all-gather.2
  66.4 62.4 all-gather.4
where the time goes:
time: 196 us
  blocking collectives  68.3 us (35%)
  waiting for transfers between devices  55.6 us (28%)
  starting transfers between devices  24.5 us (12%)
  local copies, waits for them, and re-layouts  17.5 us (9%)
  between operations  13.8 us (7%)
  matrix products  11.9 us (6%)
  other arithmetic  4.01 us (2%)
    psum x5, blocking collectives, over_axes_2(): return functools.reduce(lax.psum, axes, shard)  41.7 us
    all_gather x1, waiting for transfers between devices, whole_of(): shard = lax.all_gather(shard, axis, axis=dim, tiled=True)  35.2 us
    all_gather x1, waiting for transfers between devices, rows_first(): result, at, done = (lax.all_gather(both, axis, axis=0, tiled=True), 0, [])  18.9 us
    all_to_all x1, blocking collectives, per_device(): lax.all_to_all(joined, CHAN, split_axis=2, concat_axis=1, tiled=True)  14.9 us
    all_gather x1, blocking collectives, whole_of(): shard = lax.all_gather(shard, axis, axis=dim, tiled=True)  11.8 us
    all_to_all x1, starting transfers between devices, from_everyone(): lax.all_to_all(jnp.broadcast_to(shard[None], (devices, *shard.shape)), ax...  10.1 us
    dot_general x9, matrix products, conv_taps(): jnp.einsum('oc,ncrw->norw', taps_weight[row_tap, col_tap], window, prefer...  7.3 us
    ppermute x1, starting transfers between devices, extended_3(): lax.ppermute(first, axis, [(b, a) for a, b in up])  5.31 us
  transfers between devices with their start and end apart: 7, of which 5 were waited for; matrix products, arithmetic and copies ran while one was open for 9% of the time, Pallas kernels for 0%

commit v1 on v0

--- a/solution.py
+++ b/solution.py
@@ -11,6 +11,11 @@
 CHAN = ("chan_0", "chan_1")
 BAND_CHAN = ("band_0", "band_1", "band_2", "chan_0", "chan_1")
 epsilon = 1e-05
+
+
+def exchange_gather(shard, mesh_axis, dim):
+    sent = jnp.stack([shard] * lax.axis_size(mesh_axis))
+    return jnp.concatenate(lax.all_to_all(sent, mesh_axis, 0, 0), axis=dim)
 
 
 def whole_of(shard, axes, dim):
@@ -60,7 +65,7 @@
 def rows_first(arrays, axis, dims):
     turned = [jnp.moveaxis(a, dim, 0) for a, dim in zip(arrays, dims)]
     both = jnp.concatenate([t.reshape(len(t), -1) for t in turned], axis=1)
-    result, at, done = (lax.all_gather(both, axis, axis=0, tiled=True), 0, [])
+    result, at, done = (exchange_gather(both, axis, 0), 0, [])
     for t, dim in zip(turned, dims):
         slab = result[:, at : at + t[0].size].reshape(-1, *t.shape[1:])
         done.append(jnp.moveaxis(slab, 0, dim))

time: 196 us -> 204 us (1.041)
  blocking collectives: 68.3 us -> 55.1 us
  waiting for transfers between devices: 55.6 us -> 68 us
  starting transfers between devices: 24.5 us -> 32.6 us
  matrix products: 11.9 us -> 9.78 us
    all_to_all x0 -> x2, waiting for transfers between devices: none -> 19.1 us  [the longest x1 10.5 us: exchange_gather(): return jnp.concatenate(lax.all_to_all(sent, mesh_axis, 0, 0), axis=dim)]
    all_gather x1 -> x0, waiting for transfers between devices: 18.9 us -> none  [rows_first(): result, at, done = (lax.all_gather(both, axis, axis=0, tiled=True), 0, [])]
    all_to_all x1 -> x0, blocking collectives: 14.9 us -> none  [per_device(): lax.all_to_all(joined, CHAN, split_axis=2, concat_axis=1, tiled=True)]
    ppermute x1, waiting for transfers between devices: 0.01 us -> 8.23 us  [extended_3(): lax.ppermute(first, axis, [(b, a) for a, b in up])]
    all_to_all x0 -> x2, starting transfers between devices: none -> 7.39 us  [the longest x1 3.82 us: per_device(): lax.all_to_all(joined, CHAN, split_axis=2, concat_axis=1, tiled=True)]
    ppermute x1, waiting for transfers between devices: 0.81 us -> 3.29 us  [extended_3(): lax.ppermute(last, axis, up)]
  transfers between devices with their start and end apart: 7 -> 8, of which waited for: 5 -> 7; matrix products, arithmetic and copies ran while one was open for 9% -> 7% of each run, Pallas kernels for 0% -> 0%
where the time goes in v1:
time: 204 us; the launch traced here: 203 us
  waiting for transfers between devices  68 us (33%)
  blocking collectives  55.1 us (27%)
  starting transfers between devices  32.6 us (16%)
  local copies, waits for them, and re-layouts  19.5 us (10%)
  between operations  13.8 us (7%)
  matrix products  9.78 us (5%)
  other arithmetic  4 us (2%)
    psum x5, blocking collectives, over_axes_2(): return functools.reduce(lax.psum, axes, shard)  43.5 us
    all_gather x1, waiting for transfers between devices, whole_of(): shard = lax.all_gather(shard, axis, axis=dim, tiled=True)  35.3 us
    all_gather x1, blocking collectives, whole_of(): shard = lax.all_gather(shard, axis, axis=dim, tiled=True)  11.6 us
    all_to_all x1, waiting for transfers between devices, exchange_gather(): return jnp.concatenate(lax.all_to_all(sent, mesh_axis, 0, 0), axis=dim)  10.5 us
    all_to_all x1, starting transfers between devices, from_everyone(): lax.all_to_all(jnp.broadcast_to(shard[None], (devices, *shard.shape)), ax...  10.1 us
    all_to_all x1, waiting for transfers between devices, per_device(): lax.all_to_all(joined, CHAN, split_axis=2, concat_axis=1, tiled=True)  8.61 us
    ppermute x1, waiting for transfers between devices, extended_3(): lax.ppermute(first, axis, [(b, a) for a, b in up])  8.23 us
    dot_general x9, matrix products, conv_taps(): jnp.einsum('oc,ncrw->norw', taps_weight[row_tap, col_tap], window, prefer...  6.4 us
  transfers between devices with their start and end apart: 8, of which 7 were waited for; matrix products, arithmetic and copies ran while one was open for 7% of the time, Pallas kernels for 0%

profile of v1, /device:TPU:16, one launch (start us, length us, event | category | flops | bytes accessed | tf_op | source)
XLA Modules:
  0.0 202.8 jit_solution(12916896906545350610)
XLA Ops:
  6.6 1.2 copy.110
  7.8 11.6 %all_gather.6 = bf16[2,48,8,512]{3,1,2,0:T(8,128)(2,1)} all-gather(bf16[2,24,8,512]{3,1,2,0:T(8,128)(2,1)S(1)} %copy.110), channel_id=1, replica_groups=mesh['band_0'=8,'band_1'=2,'band_2'=2,'chan_0'=4,'chan_1'=2] {'chan_1'}, dimensions={1}, use_global_device_ids=true | all-gather | bytes 1179648 | tf_op jit(solution)/shard_map/all_gather | solution.py:23
  19.5 1.9 collective-permute-start
  21.4 5.1 %collective-permute-start.1 = (bf16[2,32,1,256]{3,1,2,0:T(8,128)(2,1)S(1)}, bf16[2,32,1,256]{3,1,2,0:T(8,128)(2,1)S(1)}, u32[]{:S(2)}, u32[]{:S(2)}) collective-permute-start(bf16[2,32,1,256]{3,1,2,0:T(8,128)(2,1)S(1)} %get-tuple-element.31), channel_id=1, source_target_pairs={{8,0},{16,8},{24,16},{32,24},{40,32},{48,40},{56,48},{64,56},{72,6... | collective-permute-start | bytes 98312 | tf_op jit(solution)/shard_map/ppermute | solution.py:58
  26.6 1.5 collective-permute-done.1
  28.2 0.1 fusion.51
  28.3 0.3 pad_maximum_fusion.2
  28.8 0.3 fusion.24
  29.1 35.3 %all-gather.2.cloned.1.call-done = bf16[2,192,8,512]{3,1,2,0:T(8,128)(2,1)} async-done(((bf16[2,48,8,512]{3,1,2,0:T(8,128)(2,1)}), bf16[2,192,8,512]{3,1,2,0:T(8,128)(2,1)}) %all-gather.2.cloned.1.call-update) | async-done | bytes 3145744 | tf_op jit(solution)/shard_map/all_gather | solution.py:23
  64.4 2.7 %fusion.50 = (f32[2,32]{1,0:T(2,128)S(1)}, f32[2,32]{1,0:T(2,128)S(1)}, f32[2,32,8,512]{3,1,2,0:T(8,128)S(1)}) fusion(bf16[2,192,8,512]{3,1,2,0:T(8,128)(2,1)} %all-gather.2.cloned.1.call-done, bf16[32,192]{1,0:T(8,128)(2,1)S(1)} %copy-done.4), kind=kOutput, calls=%fused_computation.91 | convolution fusion | flops 101449600 | bytes 4207104 | tf_op jit(solution)/shard_map/oc,ncrw->norw/dot_general | solution.py:156
  67.1 0.1 reduce_sum.67
  67.4 0.1 reduce_sum.73
  67.7 0.6 broadcast_in_dim.2
  68.3 10.1 %all-to-all-start = ((f32[32,1,16]{2,1,0:T(1,128)}), f32[32,1,16]{2,1,0:T(1,128)S(1)}, u32[]{:S(2)}, u32[]{:S(2)}) async-start(f32[32,1,16]{2,1,0:T(1,128)} %broadcast_in_dim.2), calls=%async_computation | async-start | bytes 32768 | tf_op jit(solution)/shard_map/all_to_all | solution.py:29
  78.4 0.1 pad_maximum_fusion
  78.5 3.7 %copy.118 = f32[2,32,8,256,2]{1,2,4,3,0:T(8,128)} copy(f32[2,32,8,256,2]{3,1,2,0,4:T(8,128)S(1)} %pad_maximum_fusion) | data formatting | bytes 2097152 | tf_op jit(solution)/shard_map/stack | solution.py:107
  82.2 2.8 %copy.119 = f32[2,32,8,512]{3,1,2,0:T(8,128)S(1)} copy(f32[2,32,8,512]{1,2,3,0:T(8,128)} %bitcast.155) | data formatting | bytes 2097152 | tf_op jit(solution)/shard_map/reshape | solution.py:110
  85.0 0.5 all-to-all-done
  86.1 0.4 add_convert_fusion
  86.6 0.8 copy.120
  87.4 3.8 %all-to-all-start.1 = ((bf16[2,32,8,512]{3,1,0,2:T(8,128)(2,1)}), bf16[2,32,8,512]{3,1,0,2:T(8,128)(2,1)S(1)}, u32[]{:S(2)}, u32[]{:S(2)}) async-start(bf16[2,32,8,512]{3,1,0,2:T(8,128)(2,1)} %copy.120), calls=%async_computation.1 | async-start | bytes 1048576 | tf_op jit(solution)/shard_map/all_to_all | solution.py:177
  91.2 0.1 copy.126
  91.3 0.1 copy.127
  91.4 0.1 copy.128
  91.5 0.1 copy.125
  91.7 0.2 reshape.202
  91.8 0.1 concatenate.20
  91.9 8.6 %all-to-all-done.1 = bf16[2,32,8,512]{3,1,0,2:T(8,128)(2,1)S(1)} async-done(((bf16[2,32,8,512]{3,1,0,2:T(8,128)(2,1)}), bf16[2,32,8,512]{3,1,0,2:T(8,128)(2,1)S(1)}, u32[]{:S(2)}, u32[]{:S(2)}) %all-to-all-start.1) | async-done | bytes 524320 | tf_op jit(solution)/shard_map/all_to_all | solution.py:177
  100.6 1.2 stack.35
  101.7 3.6 %all-to-all-start.2 = ((bf16[8,32,2563]{2,1,0:T(8,128)(2,1)}), bf16[8,32,2563]{2,1,0:T(8,128)(2,1)S(1)}, u32[]{:S(2)}, u32[]{:S(2)}) async-start(bf16[8,32,2563]{2,1,0:T(8,128)(2,1)} %stack.35), calls=%async_computation.2 | async-start | bytes 2752512 | tf_op jit(solution)/shard_map/all_to_all | solution.py:18
  105.4 1.0 copy.122
  106.4 6.1 %collective-permute-start.3 = (bf16[2,256,1,512]{1,3,0,2:T(8,128)(2,1)}, bf16[2,256,1,512]{1,3,0,2:T(8,128)(2,1)}, u32[]{:S(2)}, u32[]{:S(2)}) collective-permute-start(bf16[2,256,1,512]{1,3,0,2:T(8,128)(2,1)} %copy.122), channel_id=1, source_target_pairs={{1,0},{2,1},{3,2},{4,3},{5,4},{6,5},{7,6},{8,7},{9,8},{10,9},{11,1... | collective-permute-start | bytes 1572872 | tf_op jit(solution)/shard_map/ppermute | solution.py:85
  112.5 1.9 collective-permute-start.2
  114.4 10.5 %all-to-all-done.2 = bf16[8,32,2563]{2,1,0:T(8,128)(2,1)S(1)} async-done(((bf16[8,32,2563]{2,1,0:T(8,128)(2,1)}), bf16[8,32,2563]{2,1,0:T(8,128)(2,1)S(1)}, u32[]{:S(2)}, u32[]{:S(2)}) %all-to-all-start.2) | async-done | bytes 1312288 | tf_op jit(solution)/shard_map/all_to_all | solution.py:18
  124.9 1.1 slice.167
  126.0 1.6 copy.129
  127.6 1.6 copy.130
  129.1 0.2 convert_reduce_fusion.2
  129.3 1.3 fusion.44
  130.6 8.2 %collective-permute-done.3 = bf16[2,256,1,512]{1,3,0,2:T(8,128)(2,1)} collective-permute-done((bf16[2,256,1,512]{1,3,0,2:T(8,128)(2,1)}, bf16[2,256,1,512]{1,3,0,2:T(8,128)(2,1)}, u32[]{:S(2)}, u32[]{:S(2)}) %collective-permute-start.3) | collective-permute-done | bytes 524320 | tf_op jit(solution)/shard_map/ppermute | solution.py:85
  138.8 3.3 %collective-permute-done.2 = bf16[2,256,1,512]{1,3,0,2:T(8,128)(2,1)} collective-permute-done((bf16[2,256,1,512]{1,3,0,2:T(8,128)(2,1)}, bf16[2,256,1,512]{1,3,0,2:T(8,128)(2,1)}, u32[]{:S(2)}, u32[]{:S(2)}) %collective-permute-start.2) | collective-permute-done | bytes 524320 | tf_op jit(solution)/shard_map/ppermute | solution.py:84
  142.1 1.7 fusion.5
  143.9 0.3 fusion.17
  144.2 0.3 fusion.18
  144.5 0.4 fusion.19
  144.9 0.3 fusion.20
  145.2 0.3 fusion.16
  145.6 1.4 fusion.27
  146.9 1.4 fusion.25
  148.3 0.7 fusion.49
  149.1 0.1 reduce_sum.91
  149.2 0.1 reduce_sum.93
  149.3 0.1 reduce_sum.94
  149.4 17.2 %all-reduce.1 = (f32[2,32]{1,0:T(2,128)S(1)}, f32[2,32]{1,0:T(2,128)S(1)}) all-reduce(f32[2,32]{1,0:T(2,128)S(1)} %reduce_sum.94, f32[2,32]{1,0:T(2,128)S(1)} %reduce_sum.91), channel_id=1, replica_groups=mesh['band_0'=8,'band_1'=2,'band_2'=2,'chan_0'=4,'chan_1'=2] {'band_0'}, use_global_device_ids=true, to_apply=%region_14.15 | all-reduce | flops 128 | bytes 1024 | tf_op jit(solution)/shard_map/psum | solution.py:97
  166.6 6.4 %all-reduce.5 = (f32[2,32]{1,0:T(2,128)S(1)}, f32[2,32]{1,0:T(2,128)S(1)}) all-reduce(f32[2,32]{1,0:T(2,128)S(1)} %get-tuple-element.12, f32[2,32]{1,0:T(2,128)S(1)} %get-tuple-element.13), channel_id=1, replica_groups=mesh['band_0'=8,'band_1'=2,'band_2'=2,'chan_0'=4,'chan_1'=2] {'band_1'}, use_global_device_ids=true, to_apply=%region_15.16 | all-reduce | flops 128 | bytes 1024 | tf_op jit(solution)/shard_map/psum | solution.py:97
  173.0 2.4 %all-reduce.4 = (f32[2,32]{1,0:T(2,128)S(1)}, f32[2,32]{1,0:T(2,128)S(1)}) all-reduce(f32[2,32]{1,0:T(2,128)S(1)} %get-tuple-element.20, f32[2,32]{1,0:T(2,128)S(1)} %get-tuple-element.21), channel_id=1, replica_groups=mesh['band_0'=8,'band_1'=2,'band_2'=2,'chan_0'=4,'chan_1'=2] {'band_2'}, use_global_device_ids=true, to_apply=%region_16.17 | all-reduce | flops 128 | bytes 1024 | tf_op jit(solution)/shard_map/psum | solution.py:97
  175.4 12.5 %all-reduce.2 = (f32[2,32]{1,0:T(2,128)S(1)}, f32[2,32]{1,0:T(2,128)S(1)}) all-reduce(f32[2,32]{1,0:T(2,128)S(1)} %get-tuple-element.18, f32[2,32]{1,0:T(2,128)S(1)} %get-tuple-element.19), channel_id=1, replica_groups=mesh['band_0'=8,'band_1'=2,'band_2'=2,'chan_0'=4,'chan_1'=2] {'chan_0'}, use_global_device_ids=true, to_apply=%region_17.18 | all-reduce | flops 128 | bytes 1024 | tf_op jit(solution)/shard_map/psum | solution.py:97
  188.0 4.9 %all-reduce.3 = (f32[2,32]{1,0:T(2,128)S(1)}, f32[2,32]{1,0:T(2,128)S(1)}) all-reduce(f32[2,32]{1,0:T(2,128)S(1)} %get-tuple-element.14, f32[2,32]{1,0:T(2,128)S(1)} %get-tuple-element.15), channel_id=1, replica_groups=mesh['band_0'=8,'band_1'=2,'band_2'=2,'chan_0'=4,'chan_1'=2] {'chan_1'}, use_global_device_ids=true, to_apply=%region_18.19 | all-reduce | flops 128 | bytes 1024 | tf_op jit(solution)/shard_map/psum | solution.py:97
  193.0 0.1 sub.59
  193.2 0.1 mul.108
  193.3 0.7 fusion.53
  194.0 0.1 exponential_reduce_fusion
  194.1 0.1 subtract_subtract_fusion
  194.2 1.7 copy.133
  (53 shorter events, 1.6 us)
Async XLA Ops:
  6.5 186.7 %copy-start = (bf16[200,256]{1,0:T(8,128)(2,1)S(1)}, bf16[200,256]{1,0:T(8,128)(2,1)}, u32[]{:S(2)}) copy-start(bf16[200,256]{1,0:T(8,128)(2,1)} %param.21) | copy-start | bytes 307204
  6.5 12.9 %copy-start.3 = (bf16[2,32,4,256]{3,2,1,0:T(4,128)(2,1)S(1)}, bf16[2,32,4,256]{3,2,1,0:T(4,128)(2,1)}, u32[]{:S(2)}) copy-start(bf16[2,32,4,256]{3,2,1,0:T(4,128)(2,1)} %param.12) | copy-start | bytes 393220
  6.5 20.0 %copy-start.9 = (bf16[32]{0:T(256)(128)(2,1)S(1)}, bf16[32]{0:T(256)(128)(2,1)}, u32[]{:S(2)}) copy-start(bf16[32]{0:T(256)(128)(2,1)} %param.14) | copy-start | bytes 196
  6.5 20.1 %copy-start.10 = (bf16[32]{0:T(256)(128)(2,1)S(1)}, bf16[32]{0:T(256)(128)(2,1)}, u32[]{:S(2)}) copy-start(bf16[32]{0:T(256)(128)(2,1)} %param.15) | copy-start | bytes 196
  6.5 57.8 %all-gather.2.cloned.1.call-start = ((), (), s32[]{:S(2)}) async-start(), calls=%async_computation.3 | async-start | bytes 3932160 | tf_op jit(solution)/shard_map/all_gather | solution.py:23
  19.5 7.1 %collective-permute-start = (bf16[2,32,1,256]{3,1,2,0:T(8,128)(2,1)S(1)}, bf16[2,32,1,256]{3,1,2,0:T(8,128)(2,1)S(1)}, u32[]{:S(2)}, u32[]{:S(2)}) collective-permute-start(bf16[2,32,1,256]{3,1,2,0:T(8,128)(2,1)S(1)} %get-tuple-element.30), channel_id=1, source_target_pairs={{0,8},{8,16},{16,24},{24,32},{32,40},{40,48},{48,56},{56,64},{64,7... | collective-permute-start | bytes 98312 | tf_op jit(solution)/shard_map/ppermute | solution.py:56
  21.4 6.7 %collective-permute-start.1 = (bf16[2,32,1,256]{3,1,2,0:T(8,128)(2,1)S(1)}, bf16[2,32,1,256]{3,1,2,0:T(8,128)(2,1)S(1)}, u32[]{:S(2)}, u32[]{:S(2)}) collective-permute-start(bf16[2,32,1,256]{3,1,2,0:T(8,128)(2,1)S(1)} %get-tuple-element.31), channel_id=1, source_target_pairs={{8,0},{16,8},{24,16},{32,24},{40,32},{48,40},{56,48},{64,56},{72,6... | collective-permute-start | bytes 98312 | tf_op jit(solution)/shard_map/ppermute | solution.py:58
  28.8 35.6 %copy-start.4 = (bf16[32,192]{1,0:T(8,128)(2,1)S(1)}, bf16[32,192]{1,0:T(8,128)(2,1)}, u32[]{:S(2)}) copy-start(bf16[32,192]{1,0:T(8,128)(2,1)} %param.13) | copy-start | bytes 36868
  68.3 17.2 %all-to-all-start = ((f32[32,1,16]{2,1,0:T(1,128)}), f32[32,1,16]{2,1,0:T(1,128)S(1)}, u32[]{:S(2)}, u32[]{:S(2)}) async-start(f32[32,1,16]{2,1,0:T(1,128)} %broadcast_in_dim.2), calls=%async_computation | async-start | bytes 32768 | tf_op jit(solution)/shard_map/all_to_all | solution.py:29
  86.5 4.7 %copy-start.6 = (bf16[32]{0:T(256)(128)(2,1)S(1)}, bf16[32]{0:T(256)(128)(2,1)}, u32[]{:S(2)}) copy-start(bf16[32]{0:T(256)(128)(2,1)} %param.17) | copy-start | bytes 196
  86.5 4.8 %copy-start.7 = (bf16[32]{0:T(256)(128)(2,1)S(1)}, bf16[32]{0:T(256)(128)(2,1)}, u32[]{:S(2)}) copy-start(bf16[32]{0:T(256)(128)(2,1)} %param.18) | copy-start | bytes 196
  86.5 4.9 %copy-start.8 = (bf16[32]{0:T(256)(128)(2,1)S(1)}, bf16[32]{0:T(256)(128)(2,1)}, u32[]{:S(2)}) copy-start(bf16[32]{0:T(256)(128)(2,1)} %param.20) | copy-start | bytes 196
  86.5 5.0 %copy-start.2 = (bf16[3,3,32,256]{3,2,1,0:T(8,128)(2,1)S(1)}, bf16[3,3,32,256]{3,2,1,0:T(8,128)(2,1)}, u32[]{:S(2)}) copy-start(bf16[3,3,32,256]{3,2,1,0:T(8,128)(2,1)} %param.16) | copy-start | bytes 442372
  86.5 5.3 %copy-start.5 = (bf16[32,256]{1,0:T(8,128)(2,1)S(1)}, bf16[32,256]{1,0:T(8,128)(2,1)}, u32[]{:S(2)}) copy-start(bf16[32,256]{1,0:T(8,128)(2,1)} %param.19) | copy-start | bytes 49156
  87.4 13.2 %all-to-all-start.1 = ((bf16[2,32,8,512]{3,1,0,2:T(8,128)(2,1)}), bf16[2,32,8,512]{3,1,0,2:T(8,128)(2,1)S(1)}, u32[]{:S(2)}, u32[]{:S(2)}) async-start(bf16[2,32,8,512]{3,1,0,2:T(8,128)(2,1)} %copy.120), calls=%async_computation.1 | async-start | bytes 1048576 | tf_op jit(solution)/shard_map/all_to_all | solution.py:177
  101.7 23.2 %all-to-all-start.2 = ((bf16[8,32,2563]{2,1,0:T(8,128)(2,1)}), bf16[8,32,2563]{2,1,0:T(8,128)(2,1)S(1)}, u32[]{:S(2)}, u32[]{:S(2)}) async-start(bf16[8,32,2563]{2,1,0:T(8,128)(2,1)} %stack.35), calls=%async_computation.2 | async-start | bytes 2752512 | tf_op jit(solution)/shard_map/all_to_all | solution.py:18
  106.4 32.5 %collective-permute-start.3 = (bf16[2,256,1,512]{1,3,0,2:T(8,128)(2,1)}, bf16[2,256,1,512]{1,3,0,2:T(8,128)(2,1)}, u32[]{:S(2)}, u32[]{:S(2)}) collective-permute-start(bf16[2,256,1,512]{1,3,0,2:T(8,128)(2,1)} %copy.122), channel_id=1, source_target_pairs={{1,0},{2,1},{3,2},{4,3},{5,4},{6,5},{7,6},{8,7},{9,8},{10,9},{11,1... | collective-permute-start | bytes 1572872 | tf_op jit(solution)/shard_map/ppermute | solution.py:85
  112.5 29.7 %collective-permute-start.2 = (bf16[2,256,1,512]{1,3,0,2:T(8,128)(2,1)}, bf16[2,256,1,512]{1,3,0,2:T(8,128)(2,1)}, u32[]{:S(2)}, u32[]{:S(2)}) collective-permute-start(bf16[2,256,1,512]{1,3,0,2:T(8,128)(2,1)} %copy.122), channel_id=1, source_target_pairs={{0,1},{1,2},{2,3},{3,4},{4,5},{5,6},{6,7},{7,8},{8,9},{9,10},{10,1... | collective-permute-start | bytes 1572872 | tf_op jit(solution)/shard_map/ppermute | solution.py:84
  130.6 13.3 %copy-start.1 = (bf16[256,3,3,256]{3,0,2,1:T(8,128)(2,1)S(1)}, bf16[256,3,3,256]{3,0,2,1:T(8,128)(2,1)}, u32[]{:S(2)}) copy-start(bf16[256,3,3,256]{3,0,2,1:T(8,128)(2,1)} %copy.130) | copy-start | bytes 3538948
Sparse Core Ops, SparseCore 0:
  19.6 44.7 all-gather.1
